TPU v7x, 32 devices: a whole 2x2x4 slice. The times are simulated.
32 devices in a mesh: rep: 8 (over y, x, core), tp: 4 (over z).
Axes of the slice: x: 2, y: 2, z: 4, core: 2. Of those that a mesh axis runs over, the one named last changes fastest.
Arguments:
- queries: bfloat16 [2048, 4096], P('rep', 'tp'), may hold values from -120 to 120
- keys_new: bfloat16 [2048, 1024], P('rep', 'tp'), may hold values from -7 to 7
- values_new: bfloat16 [2048, 1024], P('rep', 'tp'), may hold values from -6 to 6
- caches: bfloat16 [16, 2, 4096, 1024], P('rep', None, None, 'tp'), may hold values from -6 to 6
- lengths: int32 [8, 2], replicated, may hold values from 128 to 4096, as said below
- moving: int32 [8], replicated, may hold values from 0 to 1
- destination: int32 [8], replicated, may hold values from 0 to 7, each once
- out_weight: bfloat16 [4096, 4096], P('tp'), may hold values from -0.09375 to 0.09375
Outputs:
- mixed: bfloat16 [2048, 4096], P('rep', 'tp')
- held_cache: bfloat16 [16, 2, 4096, 1024], P('rep', None, None, 'tp')
Inputs may be any that keep to these rules, and one draw needn't show every extreme that they name: `lengths`: multiples of 128; in every draw some slot holds 4096 and some 128. `destination`: each replica receives exactly one failing candidate; it takes the slot that its own failing candidate leaves.
All inputs are finite; a program needn't handle non-finite values.
Results may differ from a plain program's by a relative error of at most 0.014.
Values may be sent and summed in bfloat16 or wider, within the bound.
A program may use at most 64 MiB of HBM per device.

v0:
```python
import functools
import itertools
import random

import jax
import jax.numpy as jnp
import numpy as np
from jax import lax
from jax.experimental import pallas as pl
from jax.experimental.pallas import tpu as pltpu
from jax.sharding import PartitionSpec as P

HEAD = 128
BLOCK = 512
LOG2E = 1.4426950408889634
masked_score = -1e30
BLOCK_ROWS = 64


def slot_kernel(
    scalars, source, query_t, keys_fresh, values_fresh, *rest, aliased, kv_count, group
):
    if aliased:
        rest = rest[1:]
    held, attended, cache, row_max, row_total, weighted, in_sem, out_sem = rest
    taken, target, length = scalars[0], scalars[1], scalars[2]
    rows = cache.shape[1]
    blocks = rows // BLOCK
    span = keys_fresh.shape[0]
    factor = HEAD ** (-0.5) * LOG2E

    def fetch(block, part):
        at = pl.ds(pl.multiple_of(block * BLOCK, BLOCK), BLOCK)
        return pltpu.make_async_copy(
            source.at[taken, part, at], cache.at[part, at], in_sem.at[block, part]
        )

    def put(block, part):
        at = pl.ds(pl.multiple_of(block * BLOCK, BLOCK), BLOCK)
        return pltpu.make_async_copy(
            cache.at[part, at], held.at[target, part, at], out_sem.at[block, part]
        )

    for block in range(blocks):
        for part in range(2):
            fetch(block, part).start()

    def scores_of(head, keys):
        return lax.dot_general(
            keys,
            query_t[head],
            (((1,), (0,)), ((), ())),
            preferred_element_type=jnp.float32,
        )

    def mix(values, weights):
        return lax.dot_general(
            values,
            weights.astype(jnp.bfloat16),
            (((0,), (0,)), ((), ())),
            preferred_element_type=jnp.float32,
        )

    key_at = lax.broadcasted_iota(jnp.int32, (span, group * span), 0)
    token_at = lax.broadcasted_iota(jnp.int32, (span, group * span), 1) % span
    for head in range(kv_count):
        lanes = slice(head * HEAD, (head + 1) * HEAD)
        scores = jnp.where(
            key_at <= token_at, scores_of(head, keys_fresh[:, lanes]), masked_score
        )
        new_max = jnp.max(scores, axis=0, keepdims=True)
        weights = jnp.exp2((scores - new_max) * factor)
        row_max[head] = new_max
        row_total[head] = jnp.sum(weights, axis=0, keepdims=True)
        weighted[head] = mix(values_fresh[:, lanes], weights)

    def absorb(block, masked):
        start = pl.multiple_of(block * BLOCK, BLOCK)
        at = pl.ds(start, BLOCK)
        for head in range(kv_count):
            lanes = slice(head * HEAD, (head + 1) * HEAD)
            scores = scores_of(head, cache[0, at, lanes])
            if masked:
                position = start + lax.broadcasted_iota(jnp.int32, scores.shape, 0)
                scores = jnp.where(position < length, scores, masked_score)
            old_max = row_max[head]
            new_max = jnp.maximum(old_max, jnp.max(scores, axis=0, keepdims=True))
            rescale = jnp.exp2((old_max - new_max) * factor)
            weights = jnp.exp2((scores - new_max) * factor)
            row_max[head] = new_max
            row_total[head] = row_total[head] * rescale + jnp.sum(
                weights, axis=0, keepdims=True
            )
            weighted[head] = weighted[head] * rescale + mix(cache[1, at, lanes], weights)

    def step(block, carry):
        for part in range(2):
            fetch(block, part).wait()
            put(block, part).start()
        start = block * BLOCK

        @pl.when(start + BLOCK <= length)
        def _():
            absorb(block, False)

        @pl.when((start < length) & (length < start + BLOCK))
        def _():
            absorb(block, True)

        return carry

    lax.fori_loop(0, blocks, step, 0)
    for head in range(kv_count):
        result = (weighted[head] / row_total[head]).T
        for member in range(group):
            lanes = slice((head * group + member) * HEAD, (head * group + member + 1) * HEAD)
            attended[:, lanes] = result[member * span : (member + 1) * span].astype(
                jnp.bfloat16
            )
    for block in range(blocks):
        for part in range(2):
            put(block, part).wait()


def attend_slot(scalars, source, query_t, keys_fresh, values_fresh, held, held_shape):
    kv_count, _, columns = query_t.shape
    span = keys_fresh.shape[0]
    group = columns // span
    rows, width = source.shape[2:]
    aliased = held is not None
    anywhere = pl.BlockSpec(memory_space=pl.ANY)
    vmem = pl.BlockSpec(memory_space=pltpu.VMEM)
    operands = [scalars, source, query_t, keys_fresh, values_fresh]
    in_specs = [pl.BlockSpec(memory_space=pltpu.SMEM), anywhere, vmem, vmem, vmem]
    if aliased:
        operands.append(held)
        in_specs.append(anywhere)
    blocks = rows // BLOCK
    return pl.pallas_call(
        functools.partial(slot_kernel, aliased=aliased, kv_count=kv_count, group=group),
        out_shape=(
            jax.ShapeDtypeStruct(held_shape, jnp.bfloat16),
            jax.ShapeDtypeStruct((span, kv_count * group * HEAD), jnp.bfloat16),
        ),
        in_specs=in_specs,
        out_specs=(anywhere, vmem),
        scratch_shapes=[
            pltpu.VMEM((2, rows, width), jnp.bfloat16),
            pltpu.VMEM((kv_count, 1, columns), jnp.float32),
            pltpu.VMEM((kv_count, 1, columns), jnp.float32),
            pltpu.VMEM((kv_count, HEAD, columns), jnp.float32),
            pltpu.SemaphoreType.DMA((blocks, 2)),
            pltpu.SemaphoreType.DMA((blocks, 2)),
        ],
        input_output_aliases={5: 0} if aliased else {},
        compiler_params=pltpu.CompilerParams(vmem_limit_bytes=60 * 1024 * 1024),
        cost_estimate=pl.CostEstimate(
            flops=4 * kv_count * columns * (rows + span) * HEAD,
            bytes_accessed=8 * rows * width,
            transcendentals=kv_count * columns * (rows + span),
        ),
    )(*operands)


def project_kernel(
    attended, weight, out, weight_blocks, outgoing, incoming, weight_sem, send_sem, recv_sem
):
    parts = weight_blocks.shape[0]
    own = lax.axis_index("tp")
    columns = out.shape[1]

    def load(step):
        part = lax.rem(own + step, parts)
        at = pl.ds(pl.multiple_of(part * columns, columns), columns)
        return pltpu.make_async_copy(
            weight.at[:, at], weight_blocks.at[step], weight_sem.at[step]
        )

    order = list(range(1, parts)) + [0]
    for step in order:
        load(step).start()
    barrier = pltpu.get_barrier_semaphore()
    for step in range(1, parts):
        pl.semaphore_signal(
            barrier,
            inc=1,
            device_id={"tp": lax.rem(own + step, parts)},
            device_id_type=pl.DeviceIdType.MESH,
        )

    def product(step):
        load(step).wait()
        return jnp.dot(
            attended[...], weight_blocks[step], preferred_element_type=jnp.float32
        )

    copies = []
    for step in range(1, parts):
        outgoing[step - 1] = product(step).astype(jnp.bfloat16)
        if step == 1:
            pl.semaphore_wait(barrier, parts - 1)
        copy = pltpu.make_async_remote_copy(
            src_ref=outgoing.at[step - 1],
            dst_ref=incoming.at[step - 1],
            send_sem=send_sem.at[step - 1],
            recv_sem=recv_sem.at[step - 1],
            device_id={"tp": lax.rem(own + step, parts)},
            device_id_type=pl.DeviceIdType.MESH,
        )
        copy.start()
        copies.append(copy)
    total = product(0)
    for step, copy in enumerate(copies):
        copy.wait_recv()
        total = total + incoming[step].astype(jnp.float32)
    out[...] = total.astype(jnp.bfloat16)
    for copy in copies:
        copy.wait_send()


def project(attended, out_weight, identity):
    parts = lax.axis_size("tp")
    rows, depth = attended.shape
    columns = out_weight.shape[1] // parts
    vmem = pl.BlockSpec(memory_space=pltpu.VMEM)
    return pl.pallas_call(
        project_kernel,
        out_shape=jax.ShapeDtypeStruct((rows, columns), jnp.bfloat16),
        in_specs=[vmem, pl.BlockSpec(memory_space=pl.ANY)],
        out_specs=vmem,
        scratch_shapes=[
            pltpu.VMEM((parts, depth, columns), jnp.bfloat16),
            pltpu.VMEM((parts - 1, rows, columns), jnp.bfloat16),
            pltpu.VMEM((parts - 1, rows, columns), jnp.bfloat16),
            pltpu.SemaphoreType.DMA((parts,)),
            pltpu.SemaphoreType.DMA((parts - 1,)),
            pltpu.SemaphoreType.DMA((parts - 1,)),
        ],
        compiler_params=pltpu.CompilerParams(
            collective_id=identity, has_side_effects=True, vmem_limit_bytes=60 * 1024 * 1024
        ),
        cost_estimate=pl.CostEstimate(
            flops=2 * rows * depth * columns * parts,
            bytes_accessed=2 * depth * columns * parts,
            transcendentals=0,
        ),
        name=f"project{identity}",
    )(attended, out_weight)


QUARTERS = 4
STREAMS = 4


def cut_bound(held_at):
    chips = range(4)
    loads = []
    for bit in (1, 2):
        for side in (0, bit):
            loads.append(
                sum(
                    held_at[c][d]
                    for c in chips
                    for d in chips
                    if c & bit == side and d & bit != side
                )
            )
    for c in chips:
        loads.append(sum(held_at[c][d] for d in chips if d != c))
        loads.append(sum(held_at[d][c] for d in chips if d != c))
    return max(-(-load // 2) for load in loads)


def left_hops(held_at):
    return sum(
        held_at[c][d] * (((c ^ d) & 1) + ((c ^ d) >> 1)) for c in range(4) for d in range(4)
    )


def try_moves(held_at, slots, rng, noise):
    held_at = [row[:] for row in held_at]
    moves = []
    for slot in range(slots):
        left = slots - slot
        hops = left_hops(held_at)
        if hops == 0:
            moves.append({})
            continue
        if hops > 8 * left or cut_bound(held_at) > left:
            return None
        free = [row[:] for row in held_at]
        chosen = {}
        links = [(c, link) for c in range(4) for link in (1, 2)]
        rng.shuffle(links)
        for c, link in links:
            best = None
            for d in range(4):
                if free[c][d] <= 0 or c == d:
                    continue
                if (c ^ d) == 3:
                    value = 2.0 + noise * rng.random()
                elif (c ^ d) & link:
                    value = 1.5 + 0.1 * free[c][d] + noise * rng.random()
                elif left >= 3 and free[c][d] > left - 1:
                    value = 0.5 + 1.5 * noise * rng.random()
                else:
                    continue
                if best is None or value > best[0]:
                    best = (value, d)
            if best:
                chosen[c, link] = best[1]
                free[c][best[1]] -= 1
        for (c, link), d in chosen.items():
            held_at[c][d] -= 1
            held_at[c ^ link][d] += 1
        moves.append(chosen)
    return moves if left_hops(held_at) == 0 else None


def find_moves(demand, rng, most):
    held_at = [[0] * 4 for _ in range(4)]
    for c in range(4):
        for d in demand[c]:
            held_at[c][d] += QUARTERS
    least = max(cut_bound(held_at), -(-left_hops(held_at) // 8))
    for slots in range(least, most + 1):
        for attempt in range(400):
            noise = 0.0 if attempt == 0 else (0.5 if attempt % 2 else 1.5)
            moves = try_moves(held_at, slots, rng, noise)
            if moves is not None:
                return slots, moves
    raise ValueError("no route")


def codes_of(demand, moves, most):
    ready = [[[] for _ in range(4)] for _ in range(4)]
    arriving = []
    for c in range(4):
        for place, d in enumerate(demand[c]):
            for k in range(QUARTERS):
                ready[c][d].append((place * QUARTERS + k, (c, place, k)))
    send = [[[0] * most for _ in range(2)] for _ in range(4)]
    for slot, chosen in enumerate(moves):
        arriving = []
        for (c, link), d in sorted(chosen.items()):
            code, chunk = ready[c][d].pop(0)
            send[c][link - 1][slot] = code
            arriving.append((c ^ link, d, 2 * QUARTERS + 2 * slot + link - 1, chunk))
        for c, d, code, chunk in arriving:
            ready[c][d].append((code, chunk))
    table = []
    for c in range(4):
        here = {chunk: code for code, chunk in ready[c][c]}
        items = sorted({chunk[:2] for chunk in here})
        finals = [here[item + (k,)] for item in items for k in range(QUARTERS)]
        table.append(send[c][0] + send[c][1] + finals)
    return table


@functools.lru_cache
def routes(most):
    pairs = [(a, b) for a in range(4) for b in range(a, 4)]
    rng = random.Random(1)
    place = np.zeros((len(pairs) ** 4,), np.int32)
    rows, slots = [], []
    for index, demand in enumerate(itertools.product(pairs, repeat=4)):
        flat = [d for pair in demand for d in pair]
        if any(flat.count(d) != 2 for d in range(4)):
            continue
        place[index] = len(rows)
        count, moves = find_moves(demand, rng, most)
        rows.append(codes_of(demand, moves, most))
        slots.append(count)
    return place, np.array(rows, np.int32), np.array(slots, np.int32)


def plan_kernel(lengths, moving, destination, place, rows, plan, found, line, sem, *, most):
    replicas = destination.shape[0]
    own = lax.axis_index("rep")
    chip = own // 2
    key = jnp.int32(0)
    swap = jnp.int32(0)
    for c in range(replicas // 2):
        first, second = destination[2 * c] // 2, destination[2 * c + 1] // 2
        low, high = jnp.minimum(first, second), jnp.maximum(first, second)
        key = key * 10 + low * (7 - low) // 2 + high
        swap = jnp.where(c == chip, (first > second).astype(jnp.int32), swap)
    seek = pltpu.make_async_copy(place.at[key // 128], found, sem)
    seek.start()
    anchor = jnp.int32(0)
    senders = [jnp.int32(0), jnp.int32(0)]
    for r in range(replicas):
        goal = destination[r]
        anchor = jnp.where(goal == own, r, anchor)
        senders = [
            jnp.where(goal == 2 * chip + index, r, sender)
            for index, sender in enumerate(senders)
        ]
    crossed = (senders[0] > senders[1]).astype(jnp.int32)
    leaving = moving[own]
    plan[0] = leaving
    plan[1] = lengths[own, 1 - leaving]
    plan[2] = lengths[anchor, moving[anchor]]
    seek.wait()
    fetch = pltpu.make_async_copy(rows.at[found[0, key % 128]], line, sem)
    fetch.start()
    fetch.wait()
    plan[3] = line[0, line.shape[1] - 1]
    size = 2 * most + 2 * QUARTERS
    for index in range(size):
        at = index
        if index >= 2 * most:
            final = index - 2 * most
            at = 2 * most + (final + QUARTERS * crossed) % (2 * QUARTERS)
        code = line[0, chip * size + at]
        turned = (code + QUARTERS * swap) % (2 * QUARTERS)
        plan[4 + index] = jnp.where(code < 2 * QUARTERS, turned, code)


def make_plan(lengths, moving, destination, counts):
    most = counts[-1]
    place, rows, slots = routes(most)
    lines = -(-place.size // 128)
    places = np.zeros((lines * 128,), np.int32)
    places[: place.size] = place
    table = np.zeros((rows.shape[0], 1, 128), np.int32)
    table[:, 0, : rows[0].size] = rows.reshape(rows.shape[0], -1)
    table[:, 0, 127] = np.sum(slots[:, None] > np.array(counts[:-1]), axis=1)
    anywhere = pl.BlockSpec(memory_space=pl.ANY)
    smem = pl.BlockSpec(memory_space=pltpu.SMEM)
    return pl.pallas_call(
        functools.partial(plan_kernel, most=most),
        out_shape=jax.ShapeDtypeStruct((4 + 2 * most + 2 * QUARTERS,), jnp.int32),
        in_specs=[smem, smem, smem, anywhere, anywhere],
        out_specs=smem,
        scratch_shapes=[
            pltpu.SMEM((1, 128), jnp.int32),
            pltpu.SMEM((1, 128), jnp.int32),
            pltpu.SemaphoreType.DMA,
        ],
        name="plan",
    )(lengths, moving, destination, jnp.asarray(places.reshape(lines, 1, 128)), jnp.asarray(table))


def route_kernel(
    plan,
    queries,
    keys_new,
    values_new,
    caches,
    weight,
    arrived,
    mixed,
    both,
    local,
    give,
    arr,
    stage,
    final,
    hand,
    query_t,
    row_max,
    row_total,
    weighted,
    attended,
    weight_blocks,
    outgoing,
    incoming,
    in_sem,
    give_sem,
    gave_sem,
    send_sem,
    recv_sem,
    keep_sem,
    hand_sem,
    got_sem,
    weight_sem,
    out_sem,
    mix_sem,
    *,
    slots,
    most,
):
    own = lax.axis_index("rep")
    part = lax.axis_index("tp")
    parts = weight_blocks.shape[0]
    core = own % 2
    partner = own + 1 - 2 * core
    across = (own + 2 - 4 * ((own // 2) % 2), own + 4 - 8 * (own // 4))
    rows = stage.shape[3]
    span, columns = mixed.shape[1:]
    kv_count = query_t.shape[0]
    group = query_t.shape[2] // span
    run = QUARTERS * rows
    factor = HEAD ** (-0.5) * LOG2E
    leaving = plan[0]

    def fetch(s):
        return pltpu.make_async_copy(
            caches.at[:, :, pl.ds(s * run, run)], both.at[s], in_sem.at[s]
        )

    def load(step):
        at = pl.ds(pl.multiple_of(lax.rem(part + step, parts) * columns, columns), columns)
        return pltpu.make_async_copy(
            weight.at[:, at], weight_blocks.at[step], weight_sem.at[step]
        )

    for s in range(STREAMS):
        fetch(s).start()
    barrier = pltpu.get_barrier_semaphore()
    peers = [{"rep": partner}] + [{"rep": peer} for peer in across]
    peers += [{"tp": lax.rem(part + step, parts)} for step in range(1, parts)]
    for peer in peers:
        pl.semaphore_signal(
            barrier, inc=1, device_id=peer, device_id_type=pl.DeviceIdType.MESH
        )

    def remote(src, dst, send, recv, peer):
        return pltpu.make_async_remote_copy(
            src_ref=src,
            dst_ref=dst,
            send_sem=send,
            recv_sem=recv,
            device_id=peer,
            device_id_type=pl.DeviceIdType.MESH,
        )

    def share(s):
        return remote(
            give.at[s],
            local.at[s, pl.ds(core * QUARTERS, QUARTERS)],
            give_sem.at[s],
            gave_sem.at[s],
            {"rep": partner},
        )

    def send(link, slot, s):
        return remote(
            stage.at[link, slot, s],
            arr.at[link, slot, s],
            send_sem.at[link, slot, s],
            recv_sem.at[link, slot, s],
            {"rep": across[link]},
        )

    def settle(s, half):
        return pltpu.make_async_copy(
            final.at[s, half],
            arrived.at[0, half, pl.ds(s * run, run)],
            keep_sem.at[s, half],
        )

    def deliver(s):
        return remote(
            hand.at[s],
            final.at[s, core],
            hand_sem.at[s],
            got_sem.at[s],
            {"rep": partner},
        )

    def mix(kind, step):
        return remote(
            outgoing.at[kind, step - 1],
            incoming.at[kind, step - 1],
            out_sem.at[kind, step - 1],
            mix_sem.at[kind, step - 1],
            {"tp": lax.rem(part + step, parts)},
        )

    def pick(s, upto, codes, write):
        def body(block, carry):
            at = pl.ds(pl.multiple_of(block * BLOCK_ROWS, BLOCK_ROWS), BLOCK_ROWS)
            values = [local[s, 0, at]] * len(codes)
            came = [(home, local[s, home, at]) for home in range(1, 2 * QUARTERS)]
            came += [
                (2 * QUARTERS + 2 * slot + link, arr[link, slot, s, at])
                for slot in range(upto)
                for link in range(2)
            ]
            for here, piece in came:
                values = [
                    lax.select(code == here, piece, value)
                    for code, value in zip(codes, values)
                ]
            for index, value in enumerate(values):
                write(index, block, value)
            return carry

        lax.fori_loop(0, rows // BLOCK_ROWS, body, 0)

    def share_out(s, carry):
        fetch(s).wait()

        def body(block, carry):
            k = block // (rows // BLOCK_ROWS)
            inner = pl.multiple_of(block % (rows // BLOCK_ROWS) * BLOCK_ROWS, BLOCK_ROWS)
            at = pl.ds(pl.multiple_of(block * BLOCK_ROWS, BLOCK_ROWS), BLOCK_ROWS)
            to = pl.ds(inner, BLOCK_ROWS)
            for half, into in ((1 - core, None), (core, core)):
                value = lax.select(
                    leaving == 0, both[s, 0, half, at], both[s, 1, half, at]
                )
                if into is None:
                    give[s, k, to] = value
                else:
                    local[s, core * QUARTERS + k, to] = value
            return carry

        lax.fori_loop(0, run // BLOCK_ROWS, body, 0)

        @pl.when(s == 0)
        def _():
            pl.semaphore_wait(barrier, len(peers))

        share(s).start()
        return carry

    lax.fori_loop(0, STREAMS, share_out, 0)
    for step in list(range(1, parts)) + [0]:
        load(step).start()

    def lanes_of(head):
        return slice(head * HEAD, (head + 1) * HEAD)

    def mix_values(values, weights):
        return lax.dot_general(
            values,
            weights.astype(jnp.bfloat16),
            (((0,), (0,)), ((), ())),
            preferred_element_type=jnp.float32,
        )

    def scores_of(head, keys):
        return lax.dot_general(
            keys,
            query_t[head],
            (((1,), (0,)), ((), ())),
            preferred_element_type=jnp.float32,
        )

    def fresh(slot):
        def choose(ref, lanes):
            return lax.select(slot == 0, ref[0, :, lanes], ref[1, :, lanes])

        key_at = lax.broadcasted_iota(jnp.int32, (span, group * span), 0)
        token_at = lax.broadcasted_iota(jnp.int32, (span, group * span), 1) % span
        for head in range(kv_count):
            for member in range(group):
                query_t[head, :, member * span : (member + 1) * span] = choose(
                    queries, lanes_of(head * group + member)
                ).T
            scores = jnp.where(
                key_at <= token_at, scores_of(head, choose(keys_new, lanes_of(head))), masked_score
            )
            new_max = jnp.max(scores, axis=0, keepdims=True)
            weights = jnp.exp2((scores - new_max) * factor)
            row_max[head] = new_max
            row_total[head] = jnp.sum(weights, axis=0, keepdims=True)
            weighted[head] = mix_values(choose(values_new, lanes_of(head)), weights)

    def absorb(start, length, piece):
        for head in range(kv_count):
            scores = scores_of(head, piece(0, head))
            position = start + lax.broadcasted_iota(jnp.int32, scores.shape, 0)
            scores = jnp.where(position < length, scores, masked_score)
            old_max = row_max[head]
            new_max = jnp.maximum(old_max, jnp.max(scores, axis=0, keepdims=True))
            rescale = jnp.exp2((old_max - new_max) * factor)
            weights = jnp.exp2((scores - new_max) * factor)
            row_max[head] = new_max
            row_total[head] = row_total[head] * rescale + jnp.sum(
                weights, axis=0, keepdims=True
            )
            weighted[head] = weighted[head] * rescale + mix_values(piece(1, head), weights)

    def finish():
        for head in range(kv_count):
            result = (weighted[head] / row_total[head]).T
            for member in range(group):
                attended[:, lanes_of(head * group + member)] = result[
                    member * span : (member + 1) * span
                ].astype(jnp.bfloat16)

    def spread_products(kind):
        def body(step, carry):
            if kind == 0:
                load(step).wait()
            outgoing[kind, step - 1] = jnp.dot(
                attended[...], weight_blocks[step], preferred_element_type=jnp.float32
            ).astype(jnp.bfloat16)
            mix(kind, step).start()
            return carry

        lax.fori_loop(1, parts, body, 0)
        if kind == 0:
            load(0).wait()
        return jnp.dot(attended[...], weight_blocks[0], preferred_element_type=jnp.float32)

    def collect(kind, total):
        for step in range(1, parts):
            mix(kind, step).wait_recv()
            total = total + incoming[kind, step - 1].astype(jnp.float32)
        return total.astype(jnp.bfloat16)

    staying_blocks = run // BLOCK

    def absorb_staying(s, block):
        inner = pl.multiple_of(block * BLOCK, BLOCK)
        at = pl.ds(inner, BLOCK)

        def piece(half, head):
            return lax.select(
                leaving == 0,
                both[s, 1, half, at, lanes_of(head)],
                both[s, 0, half, at, lanes_of(head)],
            )

        absorb(s * run + inner, plan[1], piece)

    for slot in range(slots):
        codes = [plan[4 + link * most + slot] for link in range(2)]

        def step_of(s, carry):
            if slot == 0:
                share(s).wait_recv()
            else:
                for link in range(2):
                    send(link, slot - 1, s).wait_recv()

            def write(link, block, value):
                at = pl.ds(pl.multiple_of(block * BLOCK_ROWS, BLOCK_ROWS), BLOCK_ROWS)
                stage[link, slot, s, at] = value

            pick(s, slot, codes, write)
            for link in range(2):
                send(link, slot, s).start()
            if 1 <= slot <= staying_blocks:
                absorb_staying(s, slot - 1)
            return carry

        lax.fori_loop(0, STREAMS, step_of, 0)
        if slot == 0:
            fresh(1 - leaving)
        if slot == staying_blocks:
            finish()
            own_total = spread_products(0)
            mixed[0] = own_total.astype(jnp.bfloat16)
            fresh(leaving)

    def last_step(s, carry):
        @pl.when(s < STREAMS)
        def _():
            for link in range(2):
                send(link, slots - 1, s).wait_recv()
            for k in range(QUARTERS):
                base = 4 + 2 * most + k
                codes = [plan[base + QUARTERS * core], plan[base + QUARTERS * (1 - core)]]

                def write(index, block, value):
                    at = pl.ds(
                        pl.multiple_of(k * rows + block * BLOCK_ROWS, BLOCK_ROWS), BLOCK_ROWS
                    )
                    if index == 0:
                        final[s, core, at] = value
                    else:
                        hand[s, at] = value

                pick(s, slots, codes, write)
            deliver(s).start()

        @pl.when(s > 0)
        def _():
            before = s - 1
            deliver(before).wait_recv()
            for half in range(2):
                settle(before, half).start()

            def body(block, carry):
                inner = pl.multiple_of(block * BLOCK, BLOCK)
                at = pl.ds(inner, BLOCK)
                absorb(
                    before * run + inner,
                    plan[2],
                    lambda half, head: final[before, half, at, lanes_of(head)],
                )
                return carry

            lax.fori_loop(0, staying_blocks, body, 0)

        return carry

    lax.fori_loop(0, STREAMS + 1, last_step, 0)
    finish()
    arrived_total = spread_products(1)
    staying_mixed = collect(0, mixed[0].astype(jnp.float32))
    arrived_mixed = collect(1, arrived_total)
    mixed[0] = lax.select(leaving == 0, arrived_mixed, staying_mixed)
    mixed[1] = lax.select(leaving == 0, staying_mixed, arrived_mixed)
    for kind in range(2):
        for step in range(1, parts):
            mix(kind, step).wait_send()

    def drain(s, carry):
        share(s).wait_send()
        for slot in range(slots):
            for link in range(2):
                send(link, slot, s).wait_send()
        for half in range(2):
            settle(s, half).wait()
        deliver(s).wait_send()
        return carry

    lax.fori_loop(0, STREAMS, drain, 0)


def route(plan, queries, keys_new, values_new, caches, out_weight, slots, most, identity):
    parts = lax.axis_size("tp")
    slot_count, span, features = queries.shape
    depth = out_weight.shape[0]
    columns = out_weight.shape[1] // parts
    halves, cache_rows, width = caches.shape[1:]
    run = cache_rows // STREAMS
    rows = run // QUARTERS
    kv_count = width // HEAD
    grouped = span * features // width
    anywhere = pl.BlockSpec(memory_space=pl.ANY)
    vmem = pl.BlockSpec(memory_space=pltpu.VMEM)
    kind = jnp.bfloat16
    dma = pltpu.SemaphoreType.DMA
    scratch = [
        pltpu.VMEM((STREAMS, slot_count, halves, run, width), kind),
        pltpu.VMEM((STREAMS, 2 * QUARTERS, rows, width), kind),
        pltpu.VMEM((STREAMS, QUARTERS, rows, width), kind),
        pltpu.VMEM((2, slots, STREAMS, rows, width), kind),
        pltpu.VMEM((2, slots, STREAMS, rows, width), kind),
        pltpu.VMEM((STREAMS, halves, run, width), kind),
        pltpu.VMEM((STREAMS, run, width), kind),
        pltpu.VMEM((kv_count, HEAD, grouped), kind),
        pltpu.VMEM((kv_count, 1, grouped), jnp.float32),
        pltpu.VMEM((kv_count, 1, grouped), jnp.float32),
        pltpu.VMEM((kv_count, HEAD, grouped), jnp.float32),
        pltpu.VMEM((span, features), kind),
        pltpu.VMEM((parts, depth, columns), kind),
        pltpu.VMEM((2, parts - 1, span, columns), kind),
        pltpu.VMEM((2, parts - 1, span, columns), kind),
        dma((STREAMS,)),
        dma((STREAMS,)),
        dma((STREAMS,)),
        dma((2, slots, STREAMS)),
        dma((2, slots, STREAMS)),
        dma((STREAMS, halves)),
        dma((STREAMS,)),
        dma((STREAMS,)),
        dma((parts,)),
        dma((2, parts - 1)),
        dma((2, parts - 1)),
    ]
    return pl.pallas_call(
        functools.partial(route_kernel, slots=slots, most=most),
        out_shape=(
            jax.ShapeDtypeStruct((1, halves, cache_rows, width), kind),
            jax.ShapeDtypeStruct((slot_count, span, columns), kind),
        ),
        in_specs=[pl.BlockSpec(memory_space=pltpu.SMEM), vmem, vmem, vmem, anywhere, anywhere],
        out_specs=(anywhere, vmem),
        scratch_shapes=scratch,
        compiler_params=pltpu.CompilerParams(
            collective_id=identity, has_side_effects=True, vmem_limit_bytes=60 * 1024 * 1024
        ),
        name=f"route{slots}",
    )(plan, queries, keys_new, values_new, caches, out_weight)


def hold_kernel(plan, caches, arrived, held, buffer, in_sem, out_sem):
    leaving = plan[0]
    staying = 1 - leaving
    pieces, halves = in_sem.shape[1:]
    size = buffer.shape[2] // pieces

    def fetch(kind, piece, half):
        at = pl.ds(piece * size, size)
        source = caches.at[staying, half, at] if kind == 0 else arrived.at[0, half, at]
        return pltpu.make_async_copy(
            source, buffer.at[kind, half, at], in_sem.at[kind, piece, half]
        )

    def put(kind, piece, half):
        at = pl.ds(piece * size, size)
        target = held.at[staying if kind == 0 else leaving, half, at]
        return pltpu.make_async_copy(
            buffer.at[kind, half, at], target, out_sem.at[kind, piece, half]
        )

    every = list(itertools.product(range(2), range(pieces), range(halves)))
    for index in every:
        fetch(*index).start()
    for index in every:
        fetch(*index).wait()
        put(*index).start()
    for index in every:
        put(*index).wait()


def hold(plan, caches, arrived):
    anywhere = pl.BlockSpec(memory_space=pl.ANY)
    halves = caches.shape[1]
    return pl.pallas_call(
        hold_kernel,
        out_shape=jax.ShapeDtypeStruct(caches.shape, caches.dtype),
        in_specs=[pl.BlockSpec(memory_space=pltpu.SMEM), anywhere, anywhere],
        out_specs=anywhere,
        scratch_shapes=[
            pltpu.VMEM(caches.shape, caches.dtype),
            pltpu.SemaphoreType.DMA((2, 4, halves)),
            pltpu.SemaphoreType.DMA((2, 4, halves)),
        ],
        name="hold",
    )(plan, caches, arrived)


def migrate(queries, keys_new, values_new, caches, lengths, moving, destination, out_weight):
    slot_count = caches.shape[0]
    span = queries.shape[0] // slot_count
    counts = (5, 6, 8)
    plan = make_plan(lengths, moving, destination, counts)

    def by_slot(array):
        return array.reshape(slot_count, span, array.shape[1])

    arrived, mixed = lax.switch(
        plan[3],
        [
            functools.partial(route, slots=slots, most=counts[-1], identity=2 + index)
            for index, slots in enumerate(counts)
        ],
        plan,
        by_slot(queries),
        by_slot(keys_new),
        by_slot(values_new),
        caches,
        out_weight,
    )
    held = hold(plan, caches, arrived)
    return mixed.reshape(slot_count * span, mixed.shape[2]), held


def on_device(queries, keys_new, values_new, caches, lengths, moving, destination, out_weight):
    replicas = lax.axis_size("rep")
    if replicas == 8:
        return migrate(
            queries, keys_new, values_new, caches, lengths, moving, destination, out_weight
        )
    own_index = lax.axis_index("rep")
    slot_count, _, cache_rows, width = caches.shape
    span = queries.shape[0] // slot_count
    kv_count = width // HEAD
    group = queries.shape[1] // width
    leaving_slot = moving[own_index]
    staying_slot = 1 - leaving_slot
    every = jnp.arange(replicas, dtype=jnp.int32)
    source_of = jnp.sum(
        jnp.where(destination[None, :] == every[:, None], every[None, :], 0), axis=1
    )
    anchor = source_of[own_index]
    incoming_length = lengths[anchor, moving[anchor]]
    staying_length = lengths[own_index, staying_slot]
    query_t = (
        queries.reshape(slot_count, span, kv_count, group, HEAD)
        .transpose(0, 2, 4, 3, 1)
        .reshape(slot_count, kv_count, HEAD, group * span)
    )
    keys_by_slot = keys_new.reshape(slot_count, span, width)
    values_by_slot = values_new.reshape(slot_count, span, width)

    def pick(array, slot):
        return lax.dynamic_index_in_dim(array, slot, 0, keepdims=False)

    held, staying_attended = attend_slot(
        jnp.stack([staying_slot, staying_slot, staying_length]),
        caches,
        pick(query_t, staying_slot),
        pick(keys_by_slot, staying_slot),
        pick(values_by_slot, staying_slot),
        None,
        caches.shape,
    )
    leaving = lax.dynamic_index_in_dim(caches, leaving_slot, 0, keepdims=False)
    piece_rows = 2 * cache_rows // replicas
    pieces = leaving.reshape(replicas, piece_rows, width)
    spread = lax.all_to_all(pieces, "rep", split_axis=0, concat_axis=0, tiled=True)
    ordered = jnp.take(spread, source_of, axis=0, mode="clip")
    arrived = lax.all_to_all(ordered, "rep", split_axis=0, concat_axis=0, tiled=True)
    arrived = arrived.reshape(1, 2, cache_rows, width)
    staying_mixed = project(staying_attended, out_weight, 0)
    held, arrived_attended = attend_slot(
        jnp.stack([jnp.zeros_like(leaving_slot), leaving_slot, incoming_length]),
        arrived,
        pick(query_t, leaving_slot),
        pick(keys_by_slot, leaving_slot),
        pick(values_by_slot, leaving_slot),
        held,
        caches.shape,
    )
    arrived_mixed = project(arrived_attended, out_weight, 1)
    mixed = jnp.where(
        leaving_slot == 0,
        jnp.concatenate([arrived_mixed, staying_mixed], axis=0),
        jnp.concatenate([staying_mixed, arrived_mixed], axis=0),
    )
    return (mixed, held)


def solution(mesh):
    in_specs = (
        P("rep", "tp"),
        P("rep", "tp"),
        P("rep", "tp"),
        P("rep", None, None, "tp"),
        P(),
        P(),
        P(),
        P("tp", None),
    )
    out_specs = (P("rep", "tp"), P("rep", None, None, "tp"))
    return jax.shard_map(
        on_device, mesh=mesh, in_specs=in_specs, out_specs=out_specs, check_vma=False
    )
```

profile of v0, /device:TPU:10, one launch (start us, length us, event | category | flops | bytes accessed | tf_op | source)
XLA Modules:
  0.0 112.4 jit_solution(8858428875095054166)
XLA Ops:
  0.6 1.3 %copy.12.lengths = s32[8,2]{1,0:T(8,128)} copy(s32[8,2]{0,1:T(2,128)} %param.17) | data formatting | bytes 128 | tf_op args[4]
  2.0 2.9 %plan.1 = s32[28]{0:T(128)S(1)} custom-call(s32[8,2]{1,0:T(8,128)} %copy.12.lengths, s32[8]{0:T(128)} %moving.1, s32[8]{0:T(128)} %destination.1, s32[79,1,128]{2,1,0:T(1,128)} %constant.10.clone.place, s32[282,1,128]{2,1,0:T(1,128)} %constant.11.clone.rows), custom_call_target="tpu_custom_call" | custom-call | tf_op jit(solution)/shard_map/plan/pallas_call | solution.py:431
  4.9 0.6 slice.3
  6.1 98.4 %conditional.1 = (bf16[1,2,4096,256]{3,2,1,0:T(8,128)(2,1)}, bf16[256,1024]{1,0:T(8,128)(2,1)S(1)}) conditional(s32[]{:T(128)} %bitcast.3, (s32[28]{0:T(128)S(1)}, bf16[2,128,1024]{2,1,0:T(8,128)(2,1)}, bf16[2,128,256]{2,1,0:T(8,128)(2,1)}, bf16[2,128,256]{2,1,0:T(8,128)(2,1)}, bf16[2,2,4096,256]{3,2,1,0:T(8,128)(2,1)}, ...), branch_computations={%region_0.0_spmd, %region_1.0_spmd, %region_2.0_spmd} | conditional | bytes 16 | solution.py:932
  6.1 98.1 %route5.1 = (bf16[1,2,4096,256]{3,2,1,0:T(8,128)(2,1)}, bf16[2,128,1024]{2,1,0:T(8,128)(2,1)S(1)}) custom-call(s32[28]{0:T(128)S(1)} %get-tuple-element.43.plan, bf16[2,128,1024]{2,1,0:T(8,128)(2,1)} %get-tuple-element.44.queries, bf16[2,128,256]{2,1,0:T(8,128)(2,1)} %get-tuple-element.45.keys_new, bf16[2,128,256]{2,1,0:T(8,128)(2,1)} %get-tuple-element.46.values_new, ...), custom_call_target="tpu_custom_call" | custom-call | tf_op jit(solution)/shard_map/cond/branch_0_fun/route5/pallas_call | solution.py:860
  104.5 7.1 %hold.1 = bf16[2,2,4096,256]{3,2,1,0:T(8,128)(2,1)} custom-call(s32[28]{0:T(128)S(1)} %plan.1, bf16[2,2,4096,256]{3,2,1,0:T(8,128)(2,1)} %caches.1, bf16[1,2,4096,256]{3,2,1,0:T(8,128)(2,1)} %get-tuple-element.72.arrived), custom_call_target="tpu_custom_call" | custom-call | tf_op jit(solution)/shard_map/hold/pallas_call | solution.py:909
  111.6 0.8 copy.20
where the time goes:
time: 113 us; the launch traced here: 112 us
  Pallas kernels  108 us (96%)
  local copies, waits for them, and re-layouts  2.72 us (2%)
  between operations  1.31 us (1%)
    pallas_call x1, Pallas kernels, route(): pl.pallas_call(functools.partial(route_kernel, slots=slots, most=most), o...  98.1 us
    pallas_call x1, Pallas kernels, hold(): pl.pallas_call(hold_kernel, out_shape=jax.ShapeDtypeStruct(caches.shape,...  7.12 us
    pallas_call x1, Pallas kernels, make_plan(): pl.pallas_call(functools.partial(plan_kernel, most=most), out_shape=jax.S...  2.87 us

commit v1 on v0

--- a/solution.py
+++ b/solution.py
@@ -374,8 +374,32 @@
     return place, np.array(rows, np.int32), np.array(slots, np.int32)
 
 
-def plan_kernel(lengths, moving, destination, place, rows, plan, found, line, sem, *, most):
+def plan_kernel(
+    lengths,
+    moving,
+    destination,
+    place,
+    rows,
+    caches,
+    plan,
+    branch,
+    held,
+    found,
+    line,
+    buffer,
+    sem,
+    in_sem,
+    out_sem,
+    *,
+    most,
+):
     replicas = destination.shape[0]
+    staying = 1 - moving[lax.axis_index("rep")]
+    fetch_piece, put_piece, every = piece_copies(
+        caches, staying, held, staying, buffer, in_sem, out_sem
+    )
+    for index in every:
+        fetch_piece(*index).start()
     own = lax.axis_index("rep")
     chip = own // 2
     key = jnp.int32(0)
@@ -399,13 +423,21 @@
     crossed = (senders[0] > senders[1]).astype(jnp.int32)
     leaving = moving[own]
     plan[0] = leaving
-    plan[1] = lengths[own, 1 - leaving]
-    plan[2] = lengths[anchor, moving[anchor]]
+    at_row = lax.broadcasted_iota(jnp.int32, lengths.shape, 0)
+    at_slot = lax.broadcasted_iota(jnp.int32, lengths.shape, 1)
+    length_of = lengths[...].astype(jnp.float32)
+
+    def look_up(row, slot):
+        here = (at_row == row) & (at_slot == slot)
+        return jnp.sum(jnp.where(here, length_of, 0.0)).astype(jnp.int32)
+
+    plan[1] = look_up(own, 1 - leaving)
+    plan[2] = look_up(anchor, moving[anchor])
     seek.wait()
     fetch = pltpu.make_async_copy(rows.at[found[0, key % 128]], line, sem)
     fetch.start()
     fetch.wait()
-    plan[3] = line[0, line.shape[1] - 1]
+    branch[0] = line[0, line.shape[1] - 1]
     size = 2 * most + 2 * QUARTERS
     for index in range(size):
         at = index
@@ -415,9 +447,33 @@
         code = line[0, chip * size + at]
         turned = (code + QUARTERS * swap) % (2 * QUARTERS)
         plan[4 + index] = jnp.where(code < 2 * QUARTERS, turned, code)
-
-
-def make_plan(lengths, moving, destination, counts):
+    for index in every:
+        fetch_piece(*index).wait()
+        put_piece(*index).start()
+    for index in every:
+        put_piece(*index).wait()
+
+
+def piece_copies(source, source_slot, held, target_slot, buffer, in_sem, out_sem):
+    pieces, halves = in_sem.shape
+    size = buffer.shape[1] // pieces
+
+    def fetch(piece, half):
+        at = pl.ds(piece * size, size)
+        return pltpu.make_async_copy(
+            source.at[source_slot, half, at], buffer.at[half, at], in_sem.at[piece, half]
+        )
+
+    def put(piece, half):
+        at = pl.ds(piece * size, size)
+        return pltpu.make_async_copy(
+            buffer.at[half, at], held.at[target_slot, half, at], out_sem.at[piece, half]
+        )
+
+    return fetch, put, list(itertools.product(range(pieces), range(halves)))
+
+
+def make_plan(lengths, moving, destination, caches, counts):
     most = counts[-1]
     place, rows, slots = routes(most)
     lines = -(-place.size // 128)
@@ -430,27 +486,51 @@
     smem = pl.BlockSpec(memory_space=pltpu.SMEM)
     return pl.pallas_call(
         functools.partial(plan_kernel, most=most),
-        out_shape=jax.ShapeDtypeStruct((4 + 2 * most + 2 * QUARTERS,), jnp.int32),
-        in_specs=[smem, smem, smem, anywhere, anywhere],
-        out_specs=smem,
+        out_shape=(
+            jax.ShapeDtypeStruct((4 + 2 * most + 2 * QUARTERS,), jnp.int32),
+            jax.ShapeDtypeStruct((1,), jnp.int32),
+            jax.ShapeDtypeStruct(caches.shape, caches.dtype),
+        ),
+        in_specs=[
+            pl.BlockSpec(memory_space=pltpu.VMEM),
+            smem,
+            smem,
+            anywhere,
+            anywhere,
+            anywhere,
+        ],
+        out_specs=(smem, smem, anywhere),
         scratch_shapes=[
             pltpu.SMEM((1, 128), jnp.int32),
             pltpu.SMEM((1, 128), jnp.int32),
+            pltpu.VMEM(caches.shape[1:], caches.dtype),
             pltpu.SemaphoreType.DMA,
+            pltpu.SemaphoreType.DMA((4, caches.shape[1])),
+            pltpu.SemaphoreType.DMA((4, caches.shape[1])),
         ],
         name="plan",
-    )(lengths, moving, destination, jnp.asarray(places.reshape(lines, 1, 128)), jnp.asarray(table))
+    )(
+        lengths,
+        moving,
+        destination,
+        jnp.asarray(places.reshape(lines, 1, 128)),
+        jnp.asarray(table),
+        caches,
+    )
 
 
 def route_kernel(
     plan,
-    queries,
-    keys_new,
-    values_new,
+    queries_from,
+    keys_from,
+    values_from,
     caches,
     weight,
     arrived,
     mixed,
+    queries,
+    keys_new,
+    values_new,
     both,
     local,
     give,
@@ -466,6 +546,8 @@
     weight_blocks,
     outgoing,
     incoming,
+    totals,
+    fresh_sem,
     in_sem,
     give_sem,
     gave_sem,
@@ -506,6 +588,12 @@
             weight.at[:, at], weight_blocks.at[step], weight_sem.at[step]
         )
 
+    fresh_copies = [
+        pltpu.make_async_copy(source, into, fresh_sem.at[index])
+        for index, (source, into) in enumerate(
+            ((queries_from, queries), (keys_from, keys_new), (values_from, values_new))
+        )
+    ]
     for s in range(STREAMS):
         fetch(s).start()
     barrier = pltpu.get_barrier_semaphore()
@@ -560,13 +648,13 @@
             {"rep": partner},
         )
 
-    def mix(kind, step):
+    def mix(kind, index, place, target):
         return remote(
-            outgoing.at[kind, step - 1],
-            incoming.at[kind, step - 1],
-            out_sem.at[kind, step - 1],
-            mix_sem.at[kind, step - 1],
-            {"tp": lax.rem(part + step, parts)},
+            outgoing.at[kind, index],
+            incoming.at[kind, place],
+            out_sem.at[kind, index],
+            mix_sem.at[kind, place],
+            {"tp": target},
         )
 
     def pick(s, upto, codes, write):
@@ -615,9 +703,12 @@
             pl.semaphore_wait(barrier, len(peers))
 
         share(s).start()
+
         return carry
 
     lax.fori_loop(0, STREAMS, share_out, 0)
+    for copy in fresh_copies:
+        copy.start()
     for step in list(range(1, parts)) + [0]:
         load(step).start()
 
@@ -683,26 +774,102 @@
                     member * span : (member + 1) * span
                 ].astype(jnp.bfloat16)
 
-    def spread_products(kind):
-        def body(step, carry):
+    relayed = parts == 4
+    low = part < parts // 2
+    edge = (part == 0) | (part == parts - 1)
+
+    def mirror(place):
+        return jnp.where(low, place, parts - 1 - place)
+
+    def product(column):
+        step = lax.rem(column - part + parts, parts)
+        return jnp.dot(
+            attended[...], weight_blocks[step], preferred_element_type=jnp.float32
+        )
+
+    def spread_direct(kind):
+        def body(index, carry):
+            column = lax.rem(part + 1 + index, parts)
             if kind == 0:
-                load(step).wait()
-            outgoing[kind, step - 1] = jnp.dot(
-                attended[...], weight_blocks[step], preferred_element_type=jnp.float32
-            ).astype(jnp.bfloat16)
-            mix(kind, step).start()
+                load(lax.rem(index + 1, parts)).wait()
+            value = product(column)
+
+            @pl.when(index < parts - 1)
+            def _():
+                outgoing[kind, index] = value.astype(jnp.bfloat16)
+                mix(kind, index, part, column).start()
+
+            @pl.when(index == parts - 1)
+            def _():
+                totals[kind] = value
+
             return carry
 
-        lax.fori_loop(1, parts, body, 0)
-        if kind == 0:
-            load(0).wait()
-        return jnp.dot(attended[...], weight_blocks[0], preferred_element_type=jnp.float32)
-
-    def collect(kind, total):
+        lax.fori_loop(0, parts, body, 0)
+
+    def collect_direct(kind):
         for step in range(1, parts):
-            mix(kind, step).wait_recv()
-            total = total + incoming[kind, step - 1].astype(jnp.float32)
-        return total.astype(jnp.bfloat16)
+            place = lax.rem(part + step, parts)
+            mix(kind, 0, place, place).wait_recv()
+            totals[kind] += incoming[kind, place].astype(jnp.float32)
+
+    def spread_relayed(kind):
+        def body(index, carry):
+            goal = jnp.where(
+                edge,
+                jnp.where(index < 2, 3 - index, jnp.where(index == 2, 0, 1)),
+                jnp.where(index == 0, 2, jnp.where(index == 1, 0, index * 2 - 3)),
+            )
+            value = product(mirror(goal))
+            slot = jnp.where(index < 2, index, 2)
+
+            @pl.when(index == 2)
+            def _():
+                totals[kind] = value
+
+            @pl.when((index != 2) & ((index < 3) | edge))
+            def _():
+                outgoing[kind, slot] = value.astype(jnp.bfloat16)
+
+            @pl.when((index == 3) & jnp.logical_not(edge))
+            def _():
+                mix(kind, 2, parts, part).wait_recv()
+                outgoing[kind, slot] = (
+                    value + incoming[kind, parts].astype(jnp.float32)
+                ).astype(jnp.bfloat16)
+
+            @pl.when(index != 2)
+            def _():
+                first = edge & (index == 0)
+                mix(
+                    kind,
+                    slot,
+                    jnp.where(first, parts, part),
+                    mirror(jnp.where(first, 1, goal)),
+                ).start()
+
+            return carry
+
+        lax.fori_loop(0, parts, body, 0)
+
+    def collect_relayed(kind):
+        def take(place):
+            mix(kind, 0, mirror(place), part).wait_recv()
+            totals[kind] += incoming[kind, mirror(place)].astype(jnp.float32)
+
+        @pl.when(edge)
+        def _():
+            take(1)
+
+        @pl.when(jnp.logical_not(edge))
+        def _():
+            take(0)
+            take(3)
+
+        take(2)
+
+    spread_arrived = spread_relayed if relayed else spread_direct
+    collect_arrived = collect_relayed if relayed else collect_direct
 
     staying_blocks = run // BLOCK
 
@@ -742,11 +909,12 @@
 
         lax.fori_loop(0, STREAMS, step_of, 0)
         if slot == 0:
+            for copy in fresh_copies:
+                copy.wait()
             fresh(1 - leaving)
         if slot == staying_blocks:
             finish()
-            own_total = spread_products(0)
-            mixed[0] = own_total.astype(jnp.bfloat16)
+            spread_direct(0)
             fresh(leaving)
 
     def last_step(s, carry):
@@ -793,14 +961,16 @@
 
     lax.fori_loop(0, STREAMS + 1, last_step, 0)
     finish()
-    arrived_total = spread_products(1)
-    staying_mixed = collect(0, mixed[0].astype(jnp.float32))
-    arrived_mixed = collect(1, arrived_total)
+    spread_arrived(1)
+    collect_direct(0)
+    staying_mixed = totals[0].astype(jnp.bfloat16)
+    collect_arrived(1)
+    arrived_mixed = totals[1].astype(jnp.bfloat16)
     mixed[0] = lax.select(leaving == 0, arrived_mixed, staying_mixed)
     mixed[1] = lax.select(leaving == 0, staying_mixed, arrived_mixed)
     for kind in range(2):
-        for step in range(1, parts):
-            mix(kind, step).wait_send()
+        for index in range(parts - 1):
+            mix(kind, index, part, lax.rem(part + 1, parts)).wait_send()
 
     def drain(s, carry):
         share(s).wait_send()
@@ -830,6 +1000,9 @@
     kind = jnp.bfloat16
     dma = pltpu.SemaphoreType.DMA
     scratch = [
+        pltpu.VMEM(queries.shape, kind),
+        pltpu.VMEM(keys_new.shape, kind),
+        pltpu.VMEM(values_new.shape, kind),
         pltpu.VMEM((STREAMS, slot_count, halves, run, width), kind),
         pltpu.VMEM((STREAMS, 2 * QUARTERS, rows, width), kind),
         pltpu.VMEM((STREAMS, QUARTERS, rows, width), kind),
@@ -844,7 +1017,9 @@
         pltpu.VMEM((span, features), kind),
         pltpu.VMEM((parts, depth, columns), kind),
         pltpu.VMEM((2, parts - 1, span, columns), kind),
-        pltpu.VMEM((2, parts - 1, span, columns), kind),
+        pltpu.VMEM((2, parts + 1, span, columns), kind),
+        pltpu.VMEM((2, span, columns), jnp.float32),
+        dma((3,)),
         dma((STREAMS,)),
         dma((STREAMS,)),
         dma((STREAMS,)),
@@ -855,7 +1030,7 @@
         dma((STREAMS,)),
         dma((parts,)),
         dma((2, parts - 1)),
-        dma((2, parts - 1)),
+        dma((2, parts + 1)),
     ]
     return pl.pallas_call(
         functools.partial(route_kernel, slots=slots, most=most),
@@ -863,7 +1038,7 @@
             jax.ShapeDtypeStruct((1, halves, cache_rows, width), kind),
             jax.ShapeDtypeStruct((slot_count, span, columns), kind),
         ),
-        in_specs=[pl.BlockSpec(memory_space=pltpu.SMEM), vmem, vmem, vmem, anywhere, anywhere],
+        in_specs=[pl.BlockSpec(memory_space=pltpu.SMEM)] + [anywhere] * 5,
         out_specs=(anywhere, vmem),
         scratch_shapes=scratch,
         compiler_params=pltpu.CompilerParams(
@@ -873,29 +1048,12 @@
     )(plan, queries, keys_new, values_new, caches, out_weight)
 
 
-def hold_kernel(plan, caches, arrived, held, buffer, in_sem, out_sem):
+def hold_kernel(plan, arrived, mixed, _, out, held, buffer, in_sem, out_sem):
     leaving = plan[0]
-    staying = 1 - leaving
-    pieces, halves = in_sem.shape[1:]
-    size = buffer.shape[2] // pieces
-
-    def fetch(kind, piece, half):
-        at = pl.ds(piece * size, size)
-        source = caches.at[staying, half, at] if kind == 0 else arrived.at[0, half, at]
-        return pltpu.make_async_copy(
-            source, buffer.at[kind, half, at], in_sem.at[kind, piece, half]
-        )
-
-    def put(kind, piece, half):
-        at = pl.ds(piece * size, size)
-        target = held.at[staying if kind == 0 else leaving, half, at]
-        return pltpu.make_async_copy(
-            buffer.at[kind, half, at], target, out_sem.at[kind, piece, half]
-        )
-
-    every = list(itertools.product(range(2), range(pieces), range(halves)))
+    fetch, put, every = piece_copies(arrived, 0, held, leaving, buffer, in_sem, out_sem)
     for index in every:
         fetch(*index).start()
+    out[...] = mixed[...]
     for index in every:
         fetch(*index).wait()
         put(*index).start()
@@ -903,34 +1061,38 @@
         put(*index).wait()
 
 
-def hold(plan, caches, arrived):
+def hold(plan, arrived, mixed, held):
     anywhere = pl.BlockSpec(memory_space=pl.ANY)
-    halves = caches.shape[1]
+    vmem = pl.BlockSpec(memory_space=pltpu.VMEM)
     return pl.pallas_call(
         hold_kernel,
-        out_shape=jax.ShapeDtypeStruct(caches.shape, caches.dtype),
-        in_specs=[pl.BlockSpec(memory_space=pltpu.SMEM), anywhere, anywhere],
-        out_specs=anywhere,
+        out_shape=(
+            jax.ShapeDtypeStruct(mixed.shape, mixed.dtype),
+            jax.ShapeDtypeStruct(held.shape, held.dtype),
+        ),
+        in_specs=[pl.BlockSpec(memory_space=pltpu.SMEM), anywhere, vmem, anywhere],
+        out_specs=(vmem, anywhere),
         scratch_shapes=[
-            pltpu.VMEM(caches.shape, caches.dtype),
-            pltpu.SemaphoreType.DMA((2, 4, halves)),
-            pltpu.SemaphoreType.DMA((2, 4, halves)),
+            pltpu.VMEM(held.shape[1:], held.dtype),
+            pltpu.SemaphoreType.DMA((4, held.shape[1])),
+            pltpu.SemaphoreType.DMA((4, held.shape[1])),
         ],
+        input_output_aliases={3: 1},
         name="hold",
-    )(plan, caches, arrived)
+    )(plan, arrived, mixed, held)
 
 
 def migrate(queries, keys_new, values_new, caches, lengths, moving, destination, out_weight):
     slot_count = caches.shape[0]
     span = queries.shape[0] // slot_count
     counts = (5, 6, 8)
-    plan = make_plan(lengths, moving, destination, counts)
+    plan, branch, held = make_plan(lengths, moving, destination, caches, counts)
 
     def by_slot(array):
         return array.reshape(slot_count, span, array.shape[1])
 
     arrived, mixed = lax.switch(
-        plan[3],
+        branch[0],
         [
             functools.partial(route, slots=slots, most=counts[-1], identity=2 + index)
             for index, slots in enumerate(counts)
@@ -942,7 +1104,7 @@
         caches,
         out_weight,
     )
-    held = hold(plan, caches, arrived)
+    mixed, held = hold(plan, arrived, mixed, held)
     return mixed.reshape(slot_count * span, mixed.shape[2]), held
 
 

time: 113 us -> 121 us (1.071)
  the two profiles are of different devices: /device:TPU:10 before, /device:TPU:0 now
where the time goes in v1:
time: 121 us
  Pallas kernels  117 us (97%)
  between operations  1.5 us (1%)
  local copies, waits for them, and re-layouts  1.43 us (1%)
    pallas_call x1, Pallas kernels, route(): pl.pallas_call(functools.partial(route_kernel, slots=slots, most=most), o...  107 us
    pallas_call x1, Pallas kernels, make_plan(): pl.pallas_call(functools.partial(plan_kernel, most=most), out_shape=(jax....  5.4 us
    pallas_call x1, Pallas kernels, hold(): pl.pallas_call(hold_kernel, out_shape=(jax.ShapeDtypeStruct(mixed.shape,...  4.91 us

profile of v1, /device:TPU:0, one launch (start us, length us, event | category | flops | bytes accessed | tf_op | source)
XLA Modules:
  0.0 120.8 jit_solution(9363479816146623172)
XLA Ops:
  0.6 0.0 copy-start.2
  0.6 0.0 copy-start.1
  0.7 0.0 copy-start
  0.7 1.4 %copy.13.lengths = s32[8,2]{1,0:T(8,128)} copy(s32[8,2]{0,1:T(2,128)} %param.17) | data formatting | bytes 128 | tf_op args[4]
  2.1 5.4 %plan.1 = (s32[28]{0:T(128)S(1)}, s32[1]{0:T(128)}, bf16[2,2,4096,256]{3,2,1,0:T(8,128)(2,1)}) custom-call(s32[8,2]{1,0:T(8,128)} %copy.13.lengths, s32[8]{0:T(128)} %moving.1, s32[8]{0:T(128)} %destination.1, s32[79,1,128]{2,1,0:T(1,128)} %constant.10.clone.place, s32[282,1,128]{2,1,0:T(1,128)} %constant.11.clone.rows, bf16[2,2,4096,256]{3,2,1,0:T(8,128)(2,1)} %caches.1), custom_call_target="tpu_custom_call" | custom-call | tf_op jit(solution)/shard_map/plan/pallas_call | solution.py:487
  8.1 0.0 copy-done.2
  8.1 0.0 copy-done.1
  8.1 0.0 copy-done
  8.1 107.6 %conditional.1 = ((bf16[1,2,4096,256]{3,2,1,0:T(8,128)(2,1)}, bf16[2,128,1024]{2,1,0:T(8,128)(2,1)S(1)})) conditional(s32[]{:T(128)} %bitcast, (s32[28]{0:T(128)S(1)}, bf16[2,128,1024]{2,1,0:T(8,128)(2,1)S(1)}, bf16[2,128,256]{2,1,0:T(8,128)(2,1)S(1)}, bf16[2,128,256]{2,1,0:T(8,128)(2,1)S(1)}, bf16[2,2,4096,256]{3,2,1,0:T(8,128)(2,1)}, ...), branch_computations={%region_0.0_spmd, %region_1.0_spmd, %region_2.0_spmd} | conditional | bytes 8 | solution.py:1094
  8.4 106.8 %route6.1 = (bf16[1,2,4096,256]{3,2,1,0:T(8,128)(2,1)}, bf16[2,128,1024]{2,1,0:T(8,128)(2,1)S(1)}) custom-call(s32[28]{0:T(128)S(1)} %get-tuple-element.42.plan, bf16[2,128,1024]{2,1,0:T(8,128)(2,1)S(1)} %get-tuple-element.43.queries_from, bf16[2,128,256]{2,1,0:T(8,128)(2,1)S(1)} %get-tuple-element.44.keys_from, ...), custom_call_target="tpu_custom_call" | custom-call | tf_op jit(solution)/shard_map/cond/branch_1_fun/route6/pallas_call | solution.py:1035
  115.7 4.9 %hold.1 = (bf16[2,128,1024]{2,1,0:T(8,128)(2,1)}, bf16[2,2,4096,256]{3,2,1,0:T(8,128)(2,1)}) custom-call(s32[28]{0:T(128)S(1)} %get-tuple-element.63.plan, bf16[1,2,4096,256]{3,2,1,0:T(8,128)(2,1)} %get-tuple-element.65.arrived, bf16[2,128,1024]{2,1,0:T(8,128)(2,1)S(1)} %get-tuple-element.66.mixed, ...), custom_call_target="tpu_custom_call", output_to_operand_aliasing={{1}: (3, {})} | custom-call | tf_op jit(solution)/shard_map/hold/pallas_call | solution.py:1067
Async XLA Ops:
  0.6 7.5 %copy-start.2 = (bf16[256,256]{1,0:T(8,128)(2,1)S(1)}, bf16[256,256]{1,0:T(8,128)(2,1)}, u32[]{:S(2)}) copy-start(bf16[256,256]{1,0:T(8,128)(2,1)} %param.15) | copy-start | bytes 393220
  0.6 7.5 %copy-start.1 = (bf16[256,256]{1,0:T(8,128)(2,1)S(1)}, bf16[256,256]{1,0:T(8,128)(2,1)}, u32[]{:S(2)}) copy-start(bf16[256,256]{1,0:T(8,128)(2,1)} %param.14) | copy-start | bytes 393220
  0.7 7.5 %copy-start = (bf16[256,1024]{1,0:T(8,128)(2,1)S(1)}, bf16[256,1024]{1,0:T(8,128)(2,1)}, u32[]{:S(2)}) copy-start(bf16[256,1024]{1,0:T(8,128)(2,1)} %param.13) | copy-start | bytes 1572868

commit v2 on v1

--- a/solution.py
+++ b/solution.py
@@ -15,6 +15,7 @@
 LOG2E = 1.4426950408889634
 masked_score = -1e30
 BLOCK_ROWS = 64
+LENGTH_STEP = 128
 
 
 def slot_kernel(
@@ -423,8 +424,8 @@
     crossed = (senders[0] > senders[1]).astype(jnp.int32)
     leaving = moving[own]
     plan[0] = leaving
-    at_row = lax.broadcasted_iota(jnp.int32, lengths.shape, 0)
-    at_slot = lax.broadcasted_iota(jnp.int32, lengths.shape, 1)
+    at_slot = lax.broadcasted_iota(jnp.int32, lengths.shape, 0)
+    at_row = lax.broadcasted_iota(jnp.int32, lengths.shape, 1)
     length_of = lengths[...].astype(jnp.float32)
 
     def look_up(row, slot):
@@ -510,7 +511,7 @@
         ],
         name="plan",
     )(
-        lengths,
+        lengths.T,
         moving,
         destination,
         jnp.asarray(places.reshape(lines, 1, 128)),
@@ -752,19 +753,26 @@
             weighted[head] = mix_values(choose(values_new, lanes_of(head)), weights)
 
     def absorb(start, length, piece):
-        for head in range(kv_count):
-            scores = scores_of(head, piece(0, head))
-            position = start + lax.broadcasted_iota(jnp.int32, scores.shape, 0)
-            scores = jnp.where(position < length, scores, masked_score)
+        every = [scores_of(head, piece(0, head)) for head in range(kv_count)]
+        for head, scores in enumerate(every):
+            parts_of = [
+                scores[at : at + LENGTH_STEP]
+                + jnp.where(start + at < length, 0.0, masked_score)
+                for at in range(0, scores.shape[0], LENGTH_STEP)
+            ]
             old_max = row_max[head]
-            new_max = jnp.maximum(old_max, jnp.max(scores, axis=0, keepdims=True))
+            new_max = old_max
+            for some in parts_of:
+                new_max = jnp.maximum(new_max, jnp.max(some, axis=0, keepdims=True))
             rescale = jnp.exp2((old_max - new_max) * factor)
-            weights = jnp.exp2((scores - new_max) * factor)
+            weights = [jnp.exp2((some - new_max) * factor) for some in parts_of]
             row_max[head] = new_max
-            row_total[head] = row_total[head] * rescale + jnp.sum(
-                weights, axis=0, keepdims=True
-            )
-            weighted[head] = weighted[head] * rescale + mix_values(piece(1, head), weights)
+            total = row_total[head] * rescale
+            for some in weights:
+                total = total + jnp.sum(some, axis=0, keepdims=True)
+            row_total[head] = total
+            rounded = jnp.concatenate([some.astype(jnp.bfloat16) for some in weights], axis=0)
+            weighted[head] = weighted[head] * rescale + mix_values(piece(1, head), rounded)
 
     def finish():
         for head in range(kv_count):
@@ -1085,7 +1093,7 @@
 def migrate(queries, keys_new, values_new, caches, lengths, moving, destination, out_weight):
     slot_count = caches.shape[0]
     span = queries.shape[0] // slot_count
-    counts = (5, 6, 8)
+    counts = (4, 5, 6, 8)
     plan, branch, held = make_plan(lengths, moving, destination, caches, counts)
 
     def by_slot(array):

time: 121 us -> 119 us (0.983)
  local copies, waits for them, and re-layouts: 1.43 us -> 0.01 us
    unnamed x7 -> x6, local copies, waits for them, and re-layouts: 1.43 us -> 0.01 us
where the time goes in v2:
time: 119 us
  Pallas kernels  117 us (98%)
  between operations  1.56 us (1%)
    pallas_call x1, Pallas kernels, route(): pl.pallas_call(functools.partial(route_kernel, slots=slots, most=most), o...  107 us
    pallas_call x1, Pallas kernels, make_plan(): pl.pallas_call(functools.partial(plan_kernel, most=most), out_shape=(jax....  5.41 us
    pallas_call x1, Pallas kernels, hold(): pl.pallas_call(hold_kernel, out_shape=(jax.ShapeDtypeStruct(mixed.shape,...  4.91 us

profile of v2, /device:TPU:0, one launch (start us, length us, event | category | flops | bytes accessed | tf_op | source)
XLA Modules:
  0.0 119.1 jit_solution(4959564230655127543)
XLA Ops:
  0.6 0.0 copy-start
  0.6 0.0 copy-start.1
  0.7 0.0 copy-start.2
  0.7 5.4 %plan.1 = (s32[28]{0:T(128)S(1)}, s32[1]{0:T(128)}, bf16[2,2,4096,256]{3,2,1,0:T(8,128)(2,1)}) custom-call(s32[2,8]{1,0:T(2,128)} %bitcast.18, s32[8]{0:T(128)} %moving.1, s32[8]{0:T(128)} %destination.1, s32[79,1,128]{2,1,0:T(1,128)} %constant.10.clone.place, s32[282,1,128]{2,1,0:T(1,128)} %constant.11.clone.rows, bf16[2,2,4096,256]{3,2,1,0:T(8,128)(2,1)} %caches.1), custom_call_target="tpu_custom_call" | custom-call | tf_op jit(solution)/shard_map/plan/pallas_call | solution.py:488
  6.7 0.0 copy-done
  6.7 0.0 copy-done.1
  6.7 0.0 copy-done.2
  6.8 107.2 %conditional.1 = ((bf16[1,2,4096,256]{3,2,1,0:T(8,128)(2,1)}, bf16[2,128,1024]{2,1,0:T(8,128)(2,1)S(1)})) conditional(s32[]{:T(128)} %bitcast.1, (s32[28]{0:T(128)S(1)}, bf16[2,128,1024]{2,1,0:T(8,128)(2,1)S(1)}, bf16[2,128,256]{2,1,0:T(8,128)(2,1)S(1)}, bf16[2,128,256]{2,1,0:T(8,128)(2,1)S(1)}, ...), branch_computations={%region_0.0_spmd, %region_1.0_spmd, %region_2.0_spmd, %region_3.0_... | conditional | bytes 8 | solution.py:1102
  7.0 106.7 %route6.1 = (bf16[1,2,4096,256]{3,2,1,0:T(8,128)(2,1)}, bf16[2,128,1024]{2,1,0:T(8,128)(2,1)S(1)}) custom-call(s32[28]{0:T(128)S(1)} %get-tuple-element.60.plan, bf16[2,128,1024]{2,1,0:T(8,128)(2,1)S(1)} %get-tuple-element.61.queries_from, bf16[2,128,256]{2,1,0:T(8,128)(2,1)S(1)} %get-tuple-element.62.keys_from, ...), custom_call_target="tpu_custom_call" | custom-call | tf_op jit(solution)/shard_map/cond/branch_2_fun/route6/pallas_call | solution.py:1043
  114.0 4.9 %hold.1 = (bf16[2,128,1024]{2,1,0:T(8,128)(2,1)}, bf16[2,2,4096,256]{3,2,1,0:T(8,128)(2,1)}) custom-call(s32[28]{0:T(128)S(1)} %get-tuple-element.81.plan, bf16[1,2,4096,256]{3,2,1,0:T(8,128)(2,1)} %get-tuple-element.83.arrived, bf16[2,128,1024]{2,1,0:T(8,128)(2,1)S(1)} %get-tuple-element.84.mixed, ...), custom_call_target="tpu_custom_call", output_to_operand_aliasing={{1}: (3, {})} | custom-call | tf_op jit(solution)/shard_map/hold/pallas_call | solution.py:1075
Async XLA Ops:
  0.6 6.1 %copy-start = (bf16[256,1024]{1,0:T(8,128)(2,1)S(1)}, bf16[256,1024]{1,0:T(8,128)(2,1)}, u32[]{:S(2)}) copy-start(bf16[256,1024]{1,0:T(8,128)(2,1)} %param.14) | copy-start | bytes 1572868
  0.6 6.1 %copy-start.1 = (bf16[256,256]{1,0:T(8,128)(2,1)S(1)}, bf16[256,256]{1,0:T(8,128)(2,1)}, u32[]{:S(2)}) copy-start(bf16[256,256]{1,0:T(8,128)(2,1)} %param.15) | copy-start | bytes 393220
  0.7 6.1 %copy-start.2 = (bf16[256,256]{1,0:T(8,128)(2,1)S(1)}, bf16[256,256]{1,0:T(8,128)(2,1)}, u32[]{:S(2)}) copy-start(bf16[256,256]{1,0:T(8,128)(2,1)} %param.16) | copy-start | bytes 393220
